TPU v7x, 32 devices: a whole 2x2x4 slice. The times are simulated.
32 devices in a mesh: row: 8 (over z, core), col: 4 (over y, x).
Axes of the slice: x: 2, y: 2, z: 4, core: 2. Of those that a mesh axis runs over, the one named last changes fastest.
Arguments:
- gradient: float32 [8192, 28672], P('row', 'col'), may hold values from -100 to 100
- residual: float32 [8192, 28672], P('row', 'col'), may hold values from -3 to 3
- q_init: float32 [4, 28672], P(None, 'col'), may hold values from -5 to 5
Outputs:
- q_factor: float32 [4, 28672], P(None, 'col')
- new_residual: float32 [8192, 28672], P('row', 'col')
All inputs are finite; a program needn't handle non-finite values.
Results may differ from a plain program's by a relative error of at most 0.00012.
Values sent between devices are 32-bit elements; how exact they have to be, the bound alone decides.
A program may use at most 128 MiB of HBM per device.

v0:
```python
import functools

import jax
import jax.numpy as jnp
from jax import lax
from jax.experimental import pallas as pl
from jax.experimental.pallas import tpu as pltpu
from jax.sharding import PartitionSpec as P

ITERS = 16
MESH = pl.DeviceIdType.MESH
LANE = 128
SUB = 8


def factor(gram):
    low = [[None] * 4 for _ in range(4)]
    for i in range(4):
        for j in range(i + 1):
            rest = gram[i][j]
            for k in range(j):
                rest = rest - low[i][k] * low[j][k]
            low[i][j] = jnp.sqrt(rest) if i == j else rest / low[j][j]
    return low


def solve(low, rows):
    found = []
    for i in range(4):
        rest = rows[i]
        for k in range(i):
            rest = rest - low[i][k] * found[k]
        found.append(rest / low[i][i])
    return found


def kernel(
    n_row, n_col, chunks,
    grad_ref, res_ref, q0_ref, q_out, p_out,
    m, slot, acc, pb, qb, p_mine, p_in, p_sum, c_mine, c_in, q_all,
    g_sem, r_sem, a_send, a_recv, b_send, b_recv, c_send, c_recv,
):
    rows, cols = m.shape
    width = q_all.shape[-1]
    tiles = width // LANE
    groups = cols // width
    chunk = rows // chunks
    me_row, me_col = lax.axis_index("row"), lax.axis_index("col")
    col_peer = lambda d: (me_row, lax.rem(me_col + d, n_col))
    row_peer = lambda d: (lax.rem(me_row + d, n_row), me_col)

    barrier = pltpu.get_barrier_semaphore()
    for d in range(1, n_col):
        pl.semaphore_signal(barrier, inc=1, device_id=col_peer(d), device_id_type=MESH)
    for d in range(1, n_row):
        pl.semaphore_signal(barrier, inc=1, device_id=row_peer(d), device_id_type=MESH)

    def grad_copy(i):
        part = pl.ds(i * chunk, chunk)
        return pltpu.make_async_copy(grad_ref.at[part], m.at[part], g_sem.at[i])

    def res_copy(i):
        part = pl.ds(i * chunk, chunk)
        return pltpu.make_async_copy(res_ref.at[part], slot.at[i % 2], r_sem.at[i % 2])

    for i in range(chunks):
        grad_copy(i).start()
        if i < 2:
            res_copy(i).start()
    for g in range(groups):
        part = slice(g * width, (g + 1) * width)
        q_now = q0_ref[:, part]
        for r in range(4):
            qb[r, :, part] = jnp.broadcast_to(q_now[r : r + 1], (SUB, width))
    c_mine[...] = jnp.zeros_like(c_mine)
    for i in range(chunks):
        grad_copy(i).wait()
        res_copy(i).wait()

        @pl.loop(0, chunk // SUB)
        def _(k):
            here = pl.ds(pl.multiple_of(i * chunk + k * SUB, SUB), SUB)
            m[here, :] += slot[i % 2, pl.ds(pl.multiple_of(k * SUB, SUB), SUB), :]

        if i + 2 < chunks:
            res_copy(i + 2).start()
    pl.semaphore_wait(barrier, n_col + n_row - 2)

    high = 32

    def iterate(step, carry):
        par = lax.rem(step, 2)

        @pl.loop(0, rows // high)
        def _(k):
            here = pl.ds(pl.multiple_of(k * high, high), high)
            totals = [jnp.zeros((high // SUB, SUB, LANE), jnp.float32)] * 4
            for c in range(cols // LANE):
                part = slice(c * LANE, (c + 1) * LANE)
                piece = m[here, part].reshape(high // SUB, SUB, LANE)
                for r in range(4):
                    totals[r] = totals[r] + piece * qb[r, :, part][None]
            for r in range(4):
                acc[r, here, :] = totals[r].reshape(high, LANE)

        for b in range(rows // LANE):
            part = slice(b * LANE, (b + 1) * LANE)
            sums = [jnp.sum(acc[r, part, :].T, axis=0, keepdims=True) for r in range(4)]
            p_mine[0, :, part] = jnp.concatenate(sums, axis=0)

        def p_copy(d):
            return pltpu.make_async_remote_copy(
                src_ref=p_mine.at[0], dst_ref=p_in.at[par, d],
                send_sem=a_send.at[d], recv_sem=a_recv.at[par, d],
                device_id=col_peer(d), device_id_type=MESH,
            )

        for d in range(1, n_col):
            p_copy(d).start()
        for d in range(1, n_col):
            p_copy(d).wait()
        p_now = p_mine[0]
        for d in range(1, n_col):
            p_now = p_now + p_in[par, d]
        p_sum[0] = p_now

        row_id = lax.broadcasted_iota(jnp.int32, (4, LANE), 0)
        lane_id = lax.broadcasted_iota(jnp.int32, (4, LANE), 1)
        corner = jnp.zeros((4, LANE), jnp.float32)
        for i in range(4):
            dots = jnp.sum(p_now * p_now[i : i + 1], axis=1, keepdims=True)
            corner = jnp.where(lane_id == i, dots, corner)
        for s in range(n_row):
            c_mine[s, :, width:] = corner
        for r in range(4):
            for b in range(rows // LANE):
                part = slice(b * LANE, (b + 1) * LANE)
                pb[r, part, :] = jnp.broadcast_to(p_now[r : r + 1, part], (LANE, LANE)).T

        @pl.loop(0, groups)
        def _(g):
            def add(k, totals):
                totals = list(totals)
                for u in range(high // SUB):
                    here = pl.ds(pl.multiple_of(k * high + u * SUB, SUB), SUB)
                    scale = [pb[r, here, :] for r in range(4)]
                    for t in range(tiles):
                        piece = m[here, pl.ds(pl.multiple_of(g * width + t * LANE, LANE), LANE)]
                        for r in range(4):
                            totals[r * tiles + t] = totals[r * tiles + t] + piece * scale[r]
                return tuple(totals)

            start = (jnp.zeros((SUB, LANE), jnp.float32),) * (4 * tiles)
            totals = lax.fori_loop(0, rows // high, add, start)
            for t in range(tiles):
                sums = [
                    jnp.sum(totals[r * tiles + t], axis=0, keepdims=True) for r in range(4)
                ]
                c_mine[g, :, t * LANE : (t + 1) * LANE] = jnp.concatenate(sums, axis=0)

        def c_copy(d):
            return pltpu.make_async_remote_copy(
                src_ref=c_mine.at[lax.rem(me_row + d, n_row)], dst_ref=c_in.at[par, d],
                send_sem=b_send.at[d], recv_sem=b_recv.at[par, d],
                device_id=row_peer(d), device_id_type=MESH,
            )

        for d in range(1, n_row):
            c_copy(d).start()
        for d in range(1, n_row):
            c_copy(d).wait()
        cross = c_mine[me_row]
        for d in range(1, n_row):
            cross = cross + c_in[par, d]
        gram = [
            [cross[i : i + 1, width + j : width + j + 1] for j in range(4)] for i in range(4)
        ]
        low = factor(gram)
        q_rows = solve(low, [cross[r : r + 1, :width] for r in range(4)])
        q_all[par, me_row] = jnp.concatenate(q_rows, axis=0)

        def q_copy(d):
            mine = q_all.at[par, me_row]
            return pltpu.make_async_remote_copy(
                src_ref=mine, dst_ref=mine,
                send_sem=c_send.at[d], recv_sem=c_recv.at[par, d],
                device_id=row_peer(d), device_id_type=MESH,
            )

        for d in range(1, n_row):
            q_copy(d).start()
        p_held = p_sum[0]
        p_rows = solve(low, [p_held[r : r + 1] for r in range(4)])
        p_out[...] = jnp.concatenate(p_rows + p_rows, axis=0)
        for d in range(1, n_row):
            q_copy(d).wait()
        for g in range(groups):
            q_now = q_all[par, g]
            for r in range(4):
                qb[r, :, g * width : (g + 1) * width] = jnp.broadcast_to(
                    q_now[r : r + 1], (SUB, width)
                )
        return carry

    lax.fori_loop(0, ITERS, iterate, 0)
    for g in range(groups):
        q_now = q_all[(ITERS - 1) % 2, g]
        q_out[:, g * width : (g + 1) * width] = jnp.concatenate([q_now, q_now], axis=0)


def shards(n_row, n_col, gradient, residual, q_init):
    rows, cols = gradient.shape
    width = -(-cols // (LANE * n_row)) * LANE
    chunks = 8
    f32 = jnp.float32
    vmem = lambda *shape: pltpu.VMEM(shape, f32)
    dma = pltpu.SemaphoreType.DMA
    q_wide, p_basis = pl.pallas_call(
        functools.partial(kernel, n_row, n_col, chunks),
        out_shape=(
            jax.ShapeDtypeStruct((SUB, cols), f32),
            jax.ShapeDtypeStruct((SUB, rows), f32),
        ),
        in_specs=[
            pl.BlockSpec(memory_space=pl.ANY),
            pl.BlockSpec(memory_space=pl.ANY),
            pl.BlockSpec(memory_space=pltpu.VMEM),
        ],
        out_specs=(
            pl.BlockSpec(memory_space=pltpu.VMEM),
            pl.BlockSpec(memory_space=pltpu.VMEM),
        ),
        scratch_shapes=[
            vmem(rows, cols),
            vmem(2, rows // chunks, cols),
            vmem(4, rows, LANE),
            vmem(4, rows, LANE),
            vmem(4, SUB, cols),
            vmem(3, 4, rows),
            vmem(3, n_col, 4, rows),
            vmem(3, 4, rows),
            vmem(n_row + 2, 4, width + LANE),
            vmem(3, n_row, 4, width + LANE),
            vmem(3, n_row, 4, width),
            dma((chunks,)),
            dma((2,)),
            dma((n_col,)),
            dma((2, n_col)),
            dma((n_row,)),
            dma((2, n_row)),
            dma((n_row,)),
            dma((2, n_row)),
        ],
        compiler_params=pltpu.CompilerParams(
            collective_id=0, has_side_effects=True, vmem_limit_bytes=60 * 1024 * 1024
        ),
    )(gradient, residual, jnp.pad(q_init, ((0, SUB - 4), (0, 0))))
    q_factor = q_wide[:4]
    left = gradient + residual
    for r in range(4):
        left = left - p_basis[r][:, None] * q_factor[r][None, :]
    return (q_factor, left)


def solution(mesh):
    in_specs = (P("row", "col"), P("row", "col"), P(None, "col"))
    out_specs = (P(None, "col"), P("row", "col"))
    body = functools.partial(shards, mesh.shape["row"], mesh.shape["col"])
    return jax.shard_map(body, mesh=mesh, in_specs=in_specs, out_specs=out_specs, check_vma=False)
```

profile of v0, /device:TPU:0, one launch (start us, length us, event | category | flops | bytes accessed | tf_op | source)
XLA Modules:
  0.0 600.3 jit_solution(5993107907958767958)
XLA Ops:
  0.6 1.6 pad.4.q0_ref
  2.2 564.5 %shard_map.50 = (f32[8,7168]{1,0:T(8,128)}, f32[8,1024]{1,0:T(8,128)}) custom-call(f32[1024,7168]{1,0:T(8,128)} %grad_ref.1, f32[1024,7168]{1,0:T(8,128)} %res_ref.1, f32[8,7168]{1,0:T(8,128)} %pad.4.q0_ref), custom_call_target="tpu_custom_call" | custom-call | tf_op jit(solution)/shard_map/pallas_call | solution.py:218
  566.8 0.9 fusion.1
  567.7 1.6 slice.31
  569.3 1.4 fusion
  570.6 29.7 %multiply_subtract_fusion = f32[1024,7168]{1,0:T(8,128)} fusion(f32[1024,7168]{1,0:T(8,128)} %grad_ref.1, f32[1024,7168]{1,0:T(8,128)} %res_ref.1, f32[7168]{0:T(1024)S(1)} %bitcast.9, f32[1024]{0:T(1024)S(1)} %bitcast.13, f32[7168]{0:T(1024)S(1)} %bitcast.10, f32[1024]{0:T(1024)S(1)} %bitcast.14, f32[7168]{0:T(1024)S(1)} %bitcast.11, f32[1024]{0:T(1024)S(1)} %bitcast.15, ...), kind=kLoop, calls=%fused_computation | loop fusion | flops 66060288 | bytes 88211456 | tf_op jit(solution)/shard_map/sub | solution.py:261
where the time goes:
time: 601 us; the launch traced here: 600 us
  Pallas kernels  565 us (94%)
  other arithmetic  29.7 us (5%)
    pallas_call x1, Pallas kernels, shards(): pl.pallas_call(functools.partial(kernel, n_row, n_col, chunks), out_shape...  565 us
    sub x1, other arithmetic, shards(): left = left - p_basis[r][:, None] * q_factor[r][None, :]  29.7 us

commit v1 on v0

v1 whole, which is shorter than its diff:
```python
import functools

import jax
import jax.numpy as jnp
from jax import lax
from jax.experimental import pallas as pl
from jax.experimental.pallas import tpu as pltpu
from jax.sharding import PartitionSpec as P

ITERS = 16
MESH = pl.DeviceIdType.MESH
LANE = 128
SLOTS = 4
f32 = jnp.float32
bf16 = jnp.bfloat16


def factor(gram):
    low = [[None] * 4 for _ in range(4)]
    for i in range(4):
        for j in range(i + 1):
            rest = gram[i][j]
            for k in range(j):
                rest = rest - low[i][k] * low[j][k]
            low[i][j] = jnp.sqrt(rest) if i == j else rest / low[j][j]
    return low


def solve(low, rows):
    found = []
    for i in range(4):
        rest = rows[i]
        for k in range(i):
            rest = rest - low[i][k] * found[k]
        found.append(rest / low[i][i])
    return found


def pieces(x):
    a = x.astype(bf16).astype(f32)
    rest = x - a
    b = rest.astype(bf16).astype(f32)
    c = rest - b
    return jnp.concatenate([a, b, c, jnp.zeros_like(x)], axis=0).astype(bf16)


def fold(acc):
    return acc[0:4] + acc[4:8] + acc[8:12]


def dot(a, b):
    return jnp.dot(a, b, preferred_element_type=f32)


def kernel(
    n_row, n_col, width, load_cols,
    grad_ref, res_ref, q0_ref, q_out, p_out,
    hi, lo, hi_t, lo_t, g_slot, r_slot,
    ps, p_acc, p_in, p_now, c_in, c_sum, g_in, low_b,
    g_sem, r_sem, p_send, p_recv, c_send, c_recv, s_send, s_recv, m_send, m_recv,
):
    rows, cols = hi.shape
    n = cols // width
    me_row, me_col = lax.axis_index("row"), lax.axis_index("col")
    col_peer = lambda d: (me_row, lax.rem(me_col + d, n_col))
    row_peer = lambda d: (lax.rem(me_row + d, n_row), me_col)
    mid = n_row // 4
    own = [max(2 * mid - 1, 0), min(2 * mid + 1, n_row - 1)]

    barrier = pltpu.get_barrier_semaphore()
    for d in range(1, n_col):
        pl.semaphore_signal(barrier, inc=1, device_id=col_peer(d), device_id_type=MESH)
    for d in range(1, n_row):
        pl.semaphore_signal(barrier, inc=1, device_id=row_peer(d), device_id_type=MESH)

    across = cols // load_cols
    blocks = (rows // LANE) * across

    def load(b):
        s = lax.rem(b, SLOTS)
        part = (
            pl.ds(pl.multiple_of((b // across) * LANE, LANE), LANE),
            pl.ds(pl.multiple_of(lax.rem(b, across) * load_cols, LANE), load_cols),
        )
        return (
            pltpu.make_async_copy(grad_ref.at[part], g_slot.at[s], g_sem.at[s]),
            pltpu.make_async_copy(res_ref.at[part], r_slot.at[s], r_sem.at[s]),
        )

    for b in range(SLOTS):
        for copy in load(b):
            copy.start()
    c_sum_rows = q0_ref[...]
    for k in range(n):
        c_sum[k] = c_sum_rows[:, k * width : (k + 1) * width]
    for i in range(4):
        for j in range(4):
            low_b[4 * i + j] = jnp.full((1, rows), 1.0 if i == j else 0.0, f32)

    @pl.loop(0, blocks)
    def _(b):
        for copy in load(b):
            copy.wait()
        s = lax.rem(b, SLOTS)
        at_row = pl.ds(pl.multiple_of((b // across) * LANE, LANE), LANE)
        at_col = pl.multiple_of(lax.rem(b, across) * load_cols, LANE)
        for t in range(load_cols // LANE):
            part = slice(t * LANE, (t + 1) * LANE)
            x = g_slot[s, :, part] + r_slot[s, :, part]
            top = x.astype(bf16)
            low = (x - top.astype(f32)).astype(bf16)
            here = pl.ds(pl.multiple_of(at_col + t * LANE, LANE), LANE)
            hi[at_row, here] = top
            lo[at_row, here] = low
            hi_t[here, at_row] = top.T
            lo_t[here, at_row] = low.T

        @pl.when(b + SLOTS < blocks)
        def _():
            for copy in load(b + SLOTS):
                copy.start()

    pl.semaphore_wait(barrier, n_col + n_row - 2)

    def to_owner(k):
        mine = c_in.at[me_row, k]
        return pltpu.make_async_remote_copy(
            src_ref=mine, dst_ref=mine, send_sem=c_send.at[k], recv_sem=c_recv.at[me_row, k],
            device_id=(own[k % 2], me_col), device_id_type=MESH,
        )

    def from_source(k, d):
        src = lax.rem(me_row + d, n_row)
        theirs = c_in.at[src, k]
        return pltpu.make_async_remote_copy(
            src_ref=theirs, dst_ref=theirs, send_sem=c_send.at[k], recv_sem=c_recv.at[src, k],
            device_id=row_peer(d), device_id_type=MESH,
        )

    def spread(k, d):
        return pltpu.make_async_remote_copy(
            src_ref=c_sum.at[k], dst_ref=c_sum.at[k], send_sem=s_send.at[k, d], recv_sem=s_recv.at[k],
            device_id=row_peer(d), device_id_type=MESH,
        )

    def gram_copy(par, d):
        mine = g_in.at[par, me_row]
        return pltpu.make_async_remote_copy(
            src_ref=mine, dst_ref=mine, send_sem=m_send.at[d], recv_sem=m_recv.at[par, d],
            device_id=row_peer(d), device_id_type=MESH,
        )

    def p_copy(par, d):
        mine = p_in.at[par, me_col]
        return pltpu.make_async_remote_copy(
            src_ref=mine, dst_ref=mine, send_sem=p_send.at[d], recv_sem=p_recv.at[par, d],
            device_id=col_peer(d), device_id_type=MESH,
        )

    is_own = [me_row == own[0], me_row == own[1]]

    def place(i):
        first = list(range(0, n, 2)) + list(range(1, n, 2))
        second = list(range(1, n, 2)) + list(range(0, n, 2))
        return jnp.where(is_own[0], first[i], jnp.where(is_own[1], second[i], i))

    def owned(k):
        even = lax.rem(k, 2) == 0
        return jnp.logical_or(
            jnp.logical_and(even, is_own[0]), jnp.logical_and(jnp.logical_not(even), is_own[1])
        )

    def settle(k):
        @pl.when(owned(k))
        def _():
            for d in range(1, n_row):
                from_source(k, d).wait_recv()
            total = c_in[0, k]
            for s in range(1, n_row):
                total = total + c_in[s, k]
            c_sum[k] = total
            for d in range(1, n_row):
                spread(k, d).start()

        @pl.when(jnp.logical_not(owned(k)))
        def _():
            spread(k, 1).wait_recv()

    def finish_sends():
        for k in range(n):
            @pl.when(is_own[k % 2])
            def _():
                for d in range(1, n_row):
                    spread(k, d).wait_send()

            @pl.when(jnp.logical_not(is_own[k % 2]))
            def _():
                to_owner(k).wait_send()

    def find_low(par):
        for d in range(1, n_row):
            gram_copy(par, d).wait()
        total = g_in[par, 0]
        for s in range(1, n_row):
            total = total + g_in[par, s]
        gram = [[total[i : i + 1, j : j + 1] for j in range(4)] for i in range(4)]
        low = factor(gram)
        for i in range(4):
            for j in range(i + 1):
                low_b[4 * i + j] = jnp.broadcast_to(low[i][j], (1, rows))

    def low_of(lanes):
        return [[low_b[4 * i + j, :, :lanes] for j in range(i + 1)] for i in range(4)]

    def iterate(step, carry):
        par = lax.rem(step, 2)
        p_acc[...] = jnp.zeros_like(p_acc)
        for i in range(n):
            k = place(i)

            @pl.when(step > 0)
            def _():
                settle(k)

            q_now = pieces(c_sum[k])
            here = pl.ds(pl.multiple_of(k * width, width), width)
            p_acc[...] += dot(q_now, hi_t[here, :]) + dot(q_now, lo_t[here, :])
            if i == min(1, n - 1):

                @pl.when(step > 0)
                def _():
                    find_low(lax.rem(step + 1, 2))

        p_in[par, me_col] = fold(p_acc[...])
        for d in range(1, n_col):
            p_copy(par, d).start()

        @pl.when(step > 0)
        def _():
            finish_sends()

        for d in range(1, n_col):
            p_copy(par, d).wait()
        total = p_in[par, 0]
        for c in range(1, n_col):
            total = total + p_in[par, c]
        p_rows = solve(low_of(rows), [total[r : r + 1] for r in range(4)])
        p_new = jnp.concatenate(p_rows, axis=0)
        p_now[...] = p_new
        ps[...] = pieces(p_new)

        lane_id = lax.broadcasted_iota(jnp.int32, (4, LANE), 1)
        corner = jnp.zeros((4, LANE), f32)
        for i in range(4):
            dots = jnp.sum(p_new * p_new[i : i + 1], axis=1, keepdims=True)
            corner = jnp.where(lane_id == i, dots, corner)
        g_in[par, me_row] = corner

        for k in range(n):
            part = slice(k * width, (k + 1) * width)
            acc = dot(ps[...], hi[:, part]) + dot(ps[...], lo[:, part])
            c_in[me_row, k] = fold(acc)

            @pl.when(jnp.logical_not(is_own[k % 2]))
            def _():
                to_owner(k).start()

            if k == 0:
                for d in range(1, n_row):
                    gram_copy(par, d).start()
        return carry

    lax.fori_loop(0, ITERS, iterate, 0)
    for i in range(n):
        settle(place(i))
    find_low((ITERS - 1) % 2)
    finish_sends()
    p_rows = solve(low_of(rows), [p_now[r : r + 1] for r in range(4)])
    p_out[...] = jnp.concatenate(p_rows, axis=0)
    low = [[low_b[4 * i + j, :, :1] for j in range(i + 1)] for i in range(4)]
    for k in range(n):
        q_rows = solve(low, [c_sum[k, r : r + 1] for r in range(4)])
        q_out[:, k * width : (k + 1) * width] = jnp.concatenate(q_rows, axis=0)


def best_width(cols, most):
    return max(w for w in range(LANE, most + 1, LANE) if cols % w == 0)


def shards(n_row, n_col, gradient, residual, q_init):
    rows, cols = gradient.shape
    width = best_width(cols, max(LANE, cols // 7))
    load_cols = best_width(cols, 1024)
    n = cols // width
    vmem = lambda *shape: pltpu.VMEM(shape, f32)
    half = lambda *shape: pltpu.VMEM(shape, bf16)
    dma = pltpu.SemaphoreType.DMA
    q_factor, p_basis = pl.pallas_call(
        functools.partial(kernel, n_row, n_col, width, load_cols),
        out_shape=(
            jax.ShapeDtypeStruct((4, cols), f32),
            jax.ShapeDtypeStruct((4, rows), f32),
        ),
        in_specs=[
            pl.BlockSpec(memory_space=pl.ANY),
            pl.BlockSpec(memory_space=pl.ANY),
            pl.BlockSpec(memory_space=pltpu.VMEM),
        ],
        out_specs=(
            pl.BlockSpec(memory_space=pltpu.VMEM),
            pl.BlockSpec(memory_space=pltpu.VMEM),
        ),
        scratch_shapes=[
            half(rows, cols),
            half(rows, cols),
            half(cols, rows),
            half(cols, rows),
            vmem(SLOTS, LANE, load_cols),
            vmem(SLOTS, LANE, load_cols),
            half(16, rows),
            vmem(16, rows),
            vmem(2, n_col, 4, rows),
            vmem(4, rows),
            vmem(n_row, n, 4, width),
            vmem(n, 4, width),
            vmem(2, n_row, 4, LANE),
            vmem(16, 1, rows),
            dma((SLOTS,)),
            dma((SLOTS,)),
            dma((n_col,)),
            dma((2, n_col)),
            dma((n,)),
            dma((n_row, n)),
            dma((n, n_row)),
            dma((n,)),
            dma((n_row,)),
            dma((2, n_row)),
        ],
        compiler_params=pltpu.CompilerParams(
            collective_id=0, has_side_effects=True, vmem_limit_bytes=67043328
        ),
    )(gradient, residual, q_init)
    left = gradient + residual
    for r in range(4):
        left = left - p_basis[r][:, None] * q_factor[r][None, :]
    return (q_factor, left)


def solution(mesh):
    in_specs = (P("row", "col"), P("row", "col"), P(None, "col"))
    out_specs = (P(None, "col"), P("row", "col"))
    body = functools.partial(shards, mesh.shape["row"], mesh.shape["col"])
    return jax.shard_map(body, mesh=mesh, in_specs=in_specs, out_specs=out_specs, check_vma=False)
```

time: 601 us -> 298 us (0.50)
  Pallas kernels: 565 us -> 265 us
    pallas_call x1, Pallas kernels: 565 us -> 265 us  [shards(): pl.pallas_call(functools.partial(kernel, n_row, n_col, width, load_cols),...]
where the time goes in v1:
time: 298 us
  Pallas kernels  265 us (89%)
  other arithmetic  29.7 us (10%)
    pallas_call x1, Pallas kernels, shards(): pl.pallas_call(functools.partial(kernel, n_row, n_col, width, load_cols),...  265 us
    sub x1, other arithmetic, shards(): left = left - p_basis[r][:, None] * q_factor[r][None, :]  29.7 us

profile of v1, /device:TPU:0, one launch (start us, length us, event | category | flops | bytes accessed | tf_op | source)
XLA Modules:
  0.0 298.1 jit_solution(6488642248493478990)
XLA Ops:
  0.6 265.0 %shard_map.50 = (f32[4,7168]{1,0:T(4,128)}, f32[4,1024]{1,0:T(4,128)}) custom-call(f32[1024,7168]{1,0:T(8,128)} %grad_ref.1, f32[1024,7168]{1,0:T(8,128)} %res_ref.1, f32[4,7168]{1,0:T(4,128)} %q0_ref.1), custom_call_target="tpu_custom_call" | custom-call | tf_op jit(solution)/shard_map/pallas_call | solution.py:298
  265.6 0.9 fusion.1
  266.5 1.2 fusion
  267.7 0.0 copy-start
  267.7 29.7 %multiply_subtract_fusion = f32[1024,7168]{1,0:T(8,128)} fusion(f32[1024,7168]{1,0:T(8,128)} %grad_ref.1, f32[1024,7168]{1,0:T(8,128)} %res_ref.1, f32[7168]{0:T(1024)S(1)} %bitcast.9, f32[1024]{0:T(1024)S(1)} %bitcast.13, f32[7168]{0:T(1024)S(1)} %bitcast.10, f32[1024]{0:T(1024)S(1)} %bitcast.14, f32[7168]{0:T(1024)S(1)} %bitcast.11, f32[1024]{0:T(1024)S(1)} %bitcast.15, ...), kind=kLoop, calls=%fused_computation | loop fusion | flops 66060288 | bytes 88211456 | tf_op jit(solution)/shard_map/sub | solution.py:345
  297.5 0.0 copy-done
  297.5 0.6 copy.6
Async XLA Ops:
  267.7 29.7 %copy-start = (f32[4,7168]{1,0:T(4,128)S(1)}, f32[4,7168]{1,0:T(4,128)}, u32[]{:S(2)}) copy-start(f32[4,7168]{1,0:T(4,128)} %get-tuple-element.16) | copy-start | bytes 344068

commit v2 on v1

v2 whole, which is shorter than its diff:
```python
import functools

import jax
import jax.numpy as jnp
from jax import lax
from jax.experimental import pallas as pl
from jax.experimental.pallas import tpu as pltpu
from jax.sharding import PartitionSpec as P

ITERS = 16
MESH = pl.DeviceIdType.MESH
LANE = 128
SLOTS = 5
GROUP = 2 * LANE
f32 = jnp.float32
bf16 = jnp.bfloat16


def factor(gram):
    low = [[None] * 4 for _ in range(4)]
    for i in range(4):
        for j in range(i + 1):
            rest = gram[i][j]
            for k in range(j):
                rest = rest - low[i][k] * low[j][k]
            low[i][j] = jnp.sqrt(rest) if i == j else rest / low[j][j]
    return low


def solve(low, rows):
    found = []
    for i in range(4):
        rest = rows[i]
        for k in range(i):
            rest = rest - low[i][k] * found[k]
        found.append(rest / low[i][i])
    return found


def split(x):
    a = x.astype(bf16).astype(f32)
    rest = x - a
    b = rest.astype(bf16).astype(f32)
    return a, b, rest - b


def pieces(x):
    return jnp.concatenate([*split(x), jnp.zeros_like(x)], axis=0).astype(bf16)


def fold(acc):
    return acc[0:4] + acc[4:8] + acc[8:12]


def dot(a, b):
    return jnp.dot(a, b, preferred_element_type=f32)


def kernel(
    n_row, n_col, parts, load_cols,
    grad_ref, res_ref, q0_ref, q_out, hi, lo, left_out, right_out,
    hi_t, lo_t, g_slot, r_slot,
    qs, ps, p_acc, p_in, p_now, c_in, c_sum, g_in, low_b,
    g_sem, r_sem, p_send, p_recv, c_send, c_recv, s_send, s_recv, m_send, m_recv,
):
    rows, cols = hi.shape
    n = len(parts)
    me_row, me_col = lax.axis_index("row"), lax.axis_index("col")
    row_peer = lambda d: (lax.rem(me_row + d, n_row), me_col)
    if n_col & (n_col - 1) == 0:
        col_peer = lambda d: (me_row, me_col ^ d)
    else:
        col_peer = lambda d: (me_row, lax.rem(me_col + d, n_col))
    col_order = list(range(n_col - 1, 0, -1))
    mid = n_row // 4
    own = [max(2 * mid - 1, 0), min(2 * mid + 1, n_row - 1)]
    is_own = [me_row == own[0], me_row == own[1]]

    barrier = pltpu.get_barrier_semaphore()
    for d in range(1, n_col):
        pl.semaphore_signal(barrier, inc=1, device_id=col_peer(d), device_id_type=MESH)
    for d in range(1, n_row):
        pl.semaphore_signal(barrier, inc=1, device_id=row_peer(d), device_id_type=MESH)

    across = cols // load_cols
    blocks = (rows // LANE) * across
    group = GROUP if rows % GROUP == 0 else LANE
    per_group = (group // LANE) * across

    def load(b):
        s = lax.rem(b, SLOTS)
        part = (
            pl.ds(pl.multiple_of((b // across) * LANE, LANE), LANE),
            pl.ds(pl.multiple_of(lax.rem(b, across) * load_cols, LANE), load_cols),
        )
        return (
            pltpu.make_async_copy(grad_ref.at[part], g_slot.at[s], g_sem.at[s]),
            pltpu.make_async_copy(res_ref.at[part], r_slot.at[s], r_sem.at[s]),
        )

    for b in range(SLOTS):
        for copy in load(b):
            copy.start()
    qs[...] = pieces(q0_ref[...])
    for i in range(4):
        for j in range(4):
            low_b[4 * i + j] = jnp.full((1, rows), 1.0 if i == j else 0.0, f32)

    @pl.loop(0, rows // group)
    def _(r):
        @pl.loop(0, per_group)
        def _(u):
            b = r * per_group + u
            for copy in load(b):
                copy.wait()
            s = lax.rem(b, SLOTS)
            at_row = pl.ds(pl.multiple_of((b // across) * LANE, LANE), LANE)
            at_col = pl.multiple_of(lax.rem(b, across) * load_cols, LANE)
            for t in range(load_cols // LANE):
                part = slice(t * LANE, (t + 1) * LANE)
                x = g_slot[s, :, part] + r_slot[s, :, part]
                top = x.astype(bf16)
                low = (x - top.astype(f32)).astype(bf16)
                here = pl.ds(pl.multiple_of(at_col + t * LANE, LANE), LANE)
                hi[at_row, here] = top
                lo[at_row, here] = low
                hi_t[here, at_row] = top.T
                lo_t[here, at_row] = low.T

            @pl.when(b + SLOTS < blocks)
            def _():
                for copy in load(b + SLOTS):
                    copy.start()

        here = pl.ds(pl.multiple_of(r * group, LANE), group)
        p_acc[:, here] = dot(qs[...], hi_t[:, here]) + dot(qs[...], lo_t[:, here])

    pl.semaphore_wait(barrier, n_col + n_row - 2)

    def to_owner(k):
        mine = c_in.at[me_row, :, parts[k]]
        return pltpu.make_async_remote_copy(
            src_ref=mine, dst_ref=mine, send_sem=c_send.at[k], recv_sem=c_recv.at[me_row, k],
            device_id=(own[k % 2], me_col), device_id_type=MESH,
        )

    def from_source(k, src):
        theirs = c_in.at[src, :, parts[k]]
        return pltpu.make_async_remote_copy(
            src_ref=theirs, dst_ref=theirs, send_sem=c_send.at[k], recv_sem=c_recv.at[src, k],
            device_id=(src, me_col), device_id_type=MESH,
        )

    def spread(k, dest):
        whole = c_sum.at[:, parts[k]]
        return pltpu.make_async_remote_copy(
            src_ref=whole, dst_ref=whole, send_sem=s_send.at[k, dest], recv_sem=s_recv.at[k],
            device_id=(dest, me_col), device_id_type=MESH,
        )

    def gram_copy(par, d):
        mine = g_in.at[par, me_row]
        return pltpu.make_async_remote_copy(
            src_ref=mine, dst_ref=mine, send_sem=m_send.at[d], recv_sem=m_recv.at[par, d],
            device_id=row_peer(d), device_id_type=MESH,
        )

    def p_copy(par, d):
        mine = p_in.at[par, me_col]
        return pltpu.make_async_remote_copy(
            src_ref=mine, dst_ref=mine, send_sem=p_send.at[d], recv_sem=p_recv.at[par, d],
            device_id=col_peer(d), device_id_type=MESH,
        )

    def far_first(o):
        others = [s for s in range(n_row) if s != o]
        return sorted(others, key=lambda s: (-abs(s // 2 - o // 2), s % 2))

    def settle():
        for side in range(2):
            @pl.when(is_own[side])
            def _():
                others = far_first(own[side])
                for k in range(side, n, 2):
                    for src in reversed(others):
                        from_source(k, src).wait_recv()
                    total = c_in[0, :, parts[k]]
                    for s in range(1, n_row):
                        total = total + c_in[s, :, parts[k]]
                    c_sum[:, parts[k]] = total
                    for dest in others:
                        spread(k, dest).start()

    def arrive(k):
        @pl.when(jnp.logical_not(is_own[k % 2]))
        def _():
            spread(k, own[k % 2]).wait_recv()

    def finish_sends():
        for side in range(2):
            @pl.when(is_own[side])
            def _():
                for k in range(side, n, 2):
                    for dest in far_first(own[side]):
                        spread(k, dest).wait_send()

            @pl.when(jnp.logical_not(is_own[side]))
            def _():
                for k in range(side, n, 2):
                    to_owner(k).wait_send()

    def find_low(par):
        for d in range(1, n_row):
            gram_copy(par, d).wait()
        total = g_in[par, 0]
        for s in range(1, n_row):
            total = total + g_in[par, s]
        gram = [[total[i : i + 1, j : j + 1] for j in range(4)] for i in range(4)]
        low = factor(gram)
        for i in range(4):
            for j in range(i + 1):
                low_b[4 * i + j] = jnp.broadcast_to(low[i][j], (1, rows))

    def low_of(lanes):
        return [[low_b[4 * i + j, :, :lanes] for j in range(i + 1)] for i in range(4)]

    def iterate(step, carry):
        par = lax.rem(step, 2)

        @pl.when(step > 0)
        def _():
            settle()
            find_low(lax.rem(step + 1, 2))
            for k in range(n):
                arrive(k)
                q_now = pieces(c_sum[:, parts[k]])
                more = dot(q_now, hi_t[parts[k], :]) + dot(q_now, lo_t[parts[k], :])
                p_acc[...] = more if k == 0 else p_acc[...] + more

        p_in[par, me_col] = fold(p_acc[...])
        for d in col_order:
            p_copy(par, d).start()

        @pl.when(step > 0)
        def _():
            finish_sends()

        for d in reversed(col_order):
            p_copy(par, d).wait()
        total = p_in[par, 0]
        for c in range(1, n_col):
            total = total + p_in[par, c]
        p_rows = solve(low_of(rows), [total[r : r + 1] for r in range(4)])
        p_new = jnp.concatenate(p_rows, axis=0)
        p_now[...] = p_new
        ps[...] = pieces(p_new)

        lane_id = lax.broadcasted_iota(jnp.int32, (4, LANE), 1)
        corner = jnp.zeros((4, LANE), f32)
        for i in range(4):
            dots = jnp.sum(p_new * p_new[i : i + 1], axis=1, keepdims=True)
            corner = jnp.where(lane_id == i, dots, corner)
        g_in[par, me_row] = corner

        for k in range(n):
            acc = dot(ps[...], hi[:, parts[k]]) + dot(ps[...], lo[:, parts[k]])
            c_in[me_row, :, parts[k]] = fold(acc)

            @pl.when(jnp.logical_not(is_own[k % 2]))
            def _():
                to_owner(k).start()

            if k == 0:
                for d in range(1, n_row):
                    gram_copy(par, d).start()
        return carry

    lax.fori_loop(0, ITERS, iterate, 0)
    settle()
    find_low((ITERS - 1) % 2)
    p_rows = solve(low_of(rows), [p_now[r : r + 1] for r in range(4)])
    a, b, c = split(jnp.concatenate(p_rows, axis=0))
    zero = jnp.zeros_like(a)
    stacked = jnp.concatenate([a, a, b, b, a, c, zero, zero], axis=0)
    for t in range(rows // LANE):
        part = slice(t * LANE, (t + 1) * LANE)
        left_out[part, :] = stacked[:, part].T.astype(bf16)
    low = [[low_b[4 * i + j, :, :1] for j in range(i + 1)] for i in range(4)]
    for k in range(n):
        arrive(k)
        q_rows = solve(low, [c_sum[r : r + 1, parts[k]] for r in range(4)])
        q_new = jnp.concatenate(q_rows, axis=0)
        q_out[:, parts[k]] = q_new
        a, b, c = split(q_new)
        zero = jnp.zeros_like(a)
        right_out[:, parts[k]] = jnp.concatenate([a, b, a, b, c, a, zero, zero], axis=0).astype(bf16)
    finish_sends()


def subtract(load_cols, hi, lo, left, right, out_ref, slot, sem):
    rows, cols = hi.shape
    across = cols // load_cols
    blocks = (rows // LANE) * across

    def store(b):
        s = lax.rem(b, SLOTS)
        part = (
            pl.ds(pl.multiple_of((b // across) * LANE, LANE), LANE),
            pl.ds(pl.multiple_of(lax.rem(b, across) * load_cols, LANE), load_cols),
        )
        return pltpu.make_async_copy(slot.at[s], out_ref.at[part], sem.at[s])

    @pl.loop(0, blocks)
    def _(b):
        @pl.when(b >= SLOTS)
        def _():
            store(b - SLOTS).wait()

        at_row = pl.ds(pl.multiple_of((b // across) * LANE, LANE), LANE)
        at_col = pl.ds(pl.multiple_of(lax.rem(b, across) * load_cols, LANE), load_cols)
        product = dot(left[at_row, :], right[:, at_col])
        x = hi[at_row, at_col].astype(f32) + lo[at_row, at_col].astype(f32)
        slot[lax.rem(b, SLOTS)] = x - product
        store(b).start()

    for b in range(max(blocks - SLOTS, 0), blocks):
        store(b).wait()


def best_width(cols, most):
    return max(w for w in range(LANE, most + 1, LANE) if cols % w == 0)


def chunks(cols):
    width = best_width(cols, max(LANE, cols // 7))
    sizes = [width] * (cols // width)
    if width % (2 * LANE) == 0:
        sizes[-1:] = [width // 2] * 2
    ends = [sum(sizes[: k + 1]) for k in range(len(sizes))]
    return [slice(end - size, end) for end, size in zip(ends, sizes)]


def shards(n_row, n_col, gradient, residual, q_init):
    rows, cols = gradient.shape
    parts = chunks(cols)
    load_cols = best_width(cols, 1024)
    n = len(parts)
    vmem = lambda *shape: pltpu.VMEM(shape, f32)
    half = lambda *shape: pltpu.VMEM(shape, bf16)
    dma = pltpu.SemaphoreType.DMA
    anywhere = pl.BlockSpec(memory_space=pl.ANY)
    held = pl.BlockSpec(memory_space=pltpu.VMEM)
    q_factor, hi, lo, left, right = pl.pallas_call(
        functools.partial(kernel, n_row, n_col, parts, load_cols),
        out_shape=(
            jax.ShapeDtypeStruct((4, cols), f32),
            half(rows, cols),
            half(rows, cols),
            half(rows, 32),
            half(32, cols),
        ),
        in_specs=[anywhere, anywhere, held],
        out_specs=(held,) * 5,
        scratch_shapes=[
            half(cols, rows),
            half(cols, rows),
            vmem(SLOTS, LANE, load_cols),
            vmem(SLOTS, LANE, load_cols),
            half(16, cols),
            half(16, rows),
            vmem(16, rows),
            vmem(2, n_col, 4, rows),
            vmem(4, rows),
            vmem(n_row, 4, cols),
            vmem(4, cols),
            vmem(2, n_row, 4, LANE),
            vmem(16, 1, rows),
            dma((SLOTS,)),
            dma((SLOTS,)),
            dma((n_col,)),
            dma((2, n_col)),
            dma((n,)),
            dma((n_row, n)),
            dma((n, n_row)),
            dma((n,)),
            dma((n_row,)),
            dma((2, n_row)),
        ],
        compiler_params=pltpu.CompilerParams(
            collective_id=0, has_side_effects=True, vmem_limit_bytes=35 * 1024 * 1024
        ),
    )(gradient, residual, q_init)
    new_residual = pl.pallas_call(
        functools.partial(subtract, load_cols),
        out_shape=jax.ShapeDtypeStruct((rows, cols), f32),
        in_specs=[held] * 4,
        out_specs=anywhere,
        scratch_shapes=[vmem(SLOTS, LANE, load_cols), dma((SLOTS,))],
        compiler_params=pltpu.CompilerParams(vmem_limit_bytes=4 * 1024 * 1024),
    )(hi, lo, left, right)
    return (q_factor, new_residual)


def solution(mesh):
    in_specs = (P("row", "col"), P("row", "col"), P(None, "col"))
    out_specs = (P(None, "col"), P("row", "col"))
    body = functools.partial(shards, mesh.shape["row"], mesh.shape["col"])
    return jax.shard_map(body, mesh=mesh, in_specs=in_specs, out_specs=out_specs, check_vma=False)
```

time: 298 us -> 274 us (0.919)
  other arithmetic: 29.7 us -> 0 us
  Pallas kernels: 265 us -> 272 us
    sub x1 -> x0, other arithmetic: 29.7 us -> none  [shards(): left = left - p_basis[r][:, None] * q_factor[r][None, :]]
    pallas_call x1 -> x2, Pallas kernels: 265 us -> 272 us  [the longest x1 259 us: shards(): pl.pallas_call(functools.partial(kernel, n_row, n_col, parts, load_cols),...]
where the time goes in v2:
time: 274 us
  Pallas kernels  272 us (99%)
    pallas_call x1, Pallas kernels, shards(): pl.pallas_call(functools.partial(kernel, n_row, n_col, parts, load_cols),...  259 us
    pallas_call x1, Pallas kernels, shards(): pl.pallas_call(functools.partial(subtract, load_cols), out_shape=jax.Shap...  13.1 us

profile of v2, /device:TPU:0, one launch (start us, length us, event | category | flops | bytes accessed | tf_op | source)
XLA Modules:
  0.0 273.6 jit_solution(17232836018804260816)
XLA Ops:
  0.6 259.2 %shard_map.50 = (f32[4,7168]{1,0:T(4,128)}, bf16[1024,7168]{1,0:T(8,128)(2,1)S(1)}, bf16[1024,7168]{1,0:T(8,128)(2,1)S(1)}, bf16[1024,32]{1,0:T(8,128)(2,1)S(1)}, bf16[32,7168]{1,0:T(8,128)(2,1)S(1)}) custom-call(f32[1024,7168]{1,0:T(8,128)} %grad_ref.1, f32[1024,7168]{1,0:T(8,128)} %res_ref.1, f32[4,7168]{1,0:T(4,128)} %q0_ref.1), custom_call_target="tpu_custom_call" | custom-call | tf_op jit(solution)/shard_map/pallas_call | solution.py:353
  259.8 0.0 copy-start
  259.8 13.1 %shard_map.51 = f32[1024,7168]{1,0:T(8,128)} custom-call(bf16[1024,7168]{1,0:T(8,128)(2,1)S(1)} %get-tuple-element.8.hi, bf16[1024,7168]{1,0:T(8,128)(2,1)S(1)} %get-tuple-element.9.lo, bf16[1024,32]{1,0:T(8,128)(2,1)S(1)} %get-tuple-element.10.left, bf16[32,7168]{1,0:T(8,128)(2,1)S(1)} %get-tuple-element.11.right), custom_call_target="tpu_custom_call" | custom-call | tf_op jit(solution)/shard_map/pallas_call | solution.py:393
  272.9 0.0 copy-done
  272.9 0.6 copy.6
Async XLA Ops:
  259.8 13.1 %copy-start = (f32[4,7168]{1,0:T(4,128)S(1)}, f32[4,7168]{1,0:T(4,128)}, u32[]{:S(2)}) copy-start(f32[4,7168]{1,0:T(4,128)} %get-tuple-element.14) | copy-start | bytes 344068

commit v3 on v2

--- a/solution.py
+++ b/solution.py
@@ -12,6 +12,7 @@
 LANE = 128
 SLOTS = 5
 GROUP = 2 * LANE
+STRIP = 4 * LANE
 f32 = jnp.float32
 bf16 = jnp.bfloat16
 
@@ -86,6 +87,7 @@
     blocks = (rows // LANE) * across
     group = GROUP if rows % GROUP == 0 else LANE
     per_group = (group // LANE) * across
+    share = cols // per_group
 
     def load(b):
         s = lax.rem(b, SLOTS)
@@ -116,6 +118,10 @@
             s = lax.rem(b, SLOTS)
             at_row = pl.ds(pl.multiple_of((b // across) * LANE, LANE), LANE)
             at_col = pl.multiple_of(lax.rem(b, across) * load_cols, LANE)
+            before = pl.ds(pl.multiple_of(jnp.maximum(r - 1, 0) * group, LANE), group)
+            deep = pl.ds(pl.multiple_of(u * share, LANE), share)
+            more = dot(qs[:, deep], hi_t[deep, before]) + dot(qs[:, deep], lo_t[deep, before])
+            p_acc[:, before] = more + jnp.where(u == 0, 0.0, p_acc[:, before])
             for t in range(load_cols // LANE):
                 part = slice(t * LANE, (t + 1) * LANE)
                 x = g_slot[s, :, part] + r_slot[s, :, part]
@@ -132,9 +138,9 @@
                 for copy in load(b + SLOTS):
                     copy.start()
 
-        here = pl.ds(pl.multiple_of(r * group, LANE), group)
-        p_acc[:, here] = dot(qs[...], hi_t[:, here]) + dot(qs[...], lo_t[:, here])
-
+
+    last = slice(rows - group, rows)
+    p_acc[:, last] = dot(qs[...], hi_t[:, last]) + dot(qs[...], lo_t[:, last])
     pl.semaphore_wait(barrier, n_col + n_row - 2)
 
     def to_owner(k):
@@ -317,10 +323,13 @@
             store(b - SLOTS).wait()
 
         at_row = pl.ds(pl.multiple_of((b // across) * LANE, LANE), LANE)
-        at_col = pl.ds(pl.multiple_of(lax.rem(b, across) * load_cols, LANE), load_cols)
-        product = dot(left[at_row, :], right[:, at_col])
-        x = hi[at_row, at_col].astype(f32) + lo[at_row, at_col].astype(f32)
-        slot[lax.rem(b, SLOTS)] = x - product
+        at_col = pl.multiple_of(lax.rem(b, across) * load_cols, LANE)
+        for t in range(0, load_cols, STRIP):
+            part = slice(t, min(t + STRIP, load_cols))
+            here = pl.ds(pl.multiple_of(at_col + t, LANE), part.stop - t)
+            product = dot(left[at_row, :], right[:, here])
+            x = hi[at_row, here].astype(f32) + lo[at_row, here].astype(f32)
+            slot[lax.rem(b, SLOTS), :, part] = x - product
         store(b).start()
 
     for b in range(max(blocks - SLOTS, 0), blocks):

time: 274 us -> 271 us (0.989)
  Pallas kernels: 272 us -> 269 us
    pallas_call x1, Pallas kernels: 259 us -> 256 us  [shards(): pl.pallas_call(functools.partial(kernel, n_row, n_col, parts, load_cols),...]
where the time goes in v3:
time: 271 us; the launch traced here: 270 us
  Pallas kernels  269 us (99%)
    pallas_call x1, Pallas kernels, shards(): pl.pallas_call(functools.partial(kernel, n_row, n_col, parts, load_cols),...  256 us
    pallas_call x1, Pallas kernels, shards(): pl.pallas_call(functools.partial(subtract, load_cols), out_shape=jax.Shap...  12.8 us

profile of v3, /device:TPU:0, one launch (start us, length us, event | category | flops | bytes accessed | tf_op | source)
XLA Modules:
  0.0 270.4 jit_solution(4200340437087548437)
XLA Ops:
  0.6 256.3 %shard_map.50 = (f32[4,7168]{1,0:T(4,128)}, bf16[1024,7168]{1,0:T(8,128)(2,1)S(1)}, bf16[1024,7168]{1,0:T(8,128)(2,1)S(1)}, bf16[1024,32]{1,0:T(8,128)(2,1)S(1)}, bf16[32,7168]{1,0:T(8,128)(2,1)S(1)}) custom-call(f32[1024,7168]{1,0:T(8,128)} %grad_ref.1, f32[1024,7168]{1,0:T(8,128)} %res_ref.1, f32[4,7168]{1,0:T(4,128)} %q0_ref.1), custom_call_target="tpu_custom_call" | custom-call | tf_op jit(solution)/shard_map/pallas_call | solution.py:362
  256.9 0.0 copy-start
  256.9 12.8 %shard_map.51 = f32[1024,7168]{1,0:T(8,128)} custom-call(bf16[1024,7168]{1,0:T(8,128)(2,1)S(1)} %get-tuple-element.8.hi, bf16[1024,7168]{1,0:T(8,128)(2,1)S(1)} %get-tuple-element.9.lo, bf16[1024,32]{1,0:T(8,128)(2,1)S(1)} %get-tuple-element.10.left, bf16[32,7168]{1,0:T(8,128)(2,1)S(1)} %get-tuple-element.11.right), custom_call_target="tpu_custom_call" | custom-call | tf_op jit(solution)/shard_map/pallas_call | solution.py:402
  269.7 0.0 copy-done
  269.7 0.6 copy.6
Async XLA Ops:
  256.9 12.8 %copy-start = (f32[4,7168]{1,0:T(4,128)S(1)}, f32[4,7168]{1,0:T(4,128)}, u32[]{:S(2)}) copy-start(f32[4,7168]{1,0:T(4,128)} %get-tuple-element.14) | copy-start | bytes 344068
